TPU v7x, 32 devices: a whole 2x2x4 slice. The times are simulated.
32 devices in a mesh: grp: 2 (over y), freq: 4 (over z), beam: 2 (over x), dm: 2 (over core).
Axes of the slice: x: 2, y: 2, z: 4, core: 2. Of those that a mesh axis runs over, the one named last changes fastest.
Arguments:
- voltages: bfloat16 [4, 2048, 16, 2, 1024], P(None, ('freq', 'beam'), ('grp', 'dm')), parts along dimension 2, may hold values from -6 to 6
- grid_feed: int32 [1024], replicated, may hold values from 0 to 1023, each once
- delays: int32 [4, 2048, 256], P('freq', None, 'dm'), may hold values from 0 to 4
Outputs:
- dedispersed: float32 [4, 256, 8, 1024], P('freq', 'dm', 'grp', 'beam'), parts along dimension 2
There are 2 independent parts, one for each index of `grp`. A program takes and returns all parts, laid end to end along the dimension named above; an argument that names none is the same for every part. Nothing has to cross between parts.
Inputs may be any that keep to these rules, and one draw needn't show every extreme that they name: `grid_feed`: each feed appears once.
All inputs are finite; a program needn't handle non-finite values.
Results may differ from a plain program's by a relative error of at most 0.0034.
Values may be sent and summed in bfloat16 or wider, within the bound.
A program may use at most 128 MiB of HBM per device.

v0:
```python
import math
import jax
import jax.numpy as jnp
from jax import lax
from jax.sharding import PartitionSpec as P

GX = 4
GY = 256
FREQS = 8192


def steering_table(length, factor):
    position = jnp.arange(length, dtype=jnp.int32)
    phase_step = position[:, None] * position[None, :] % length
    phase_angle = phase_step.astype(jnp.float32) * (2.0 * math.pi / length)
    cosine = jnp.cos(phase_angle) * factor
    sine_part = jnp.sin(phase_angle) * factor
    upper_half = jnp.concatenate([cosine, -sine_part], axis=1)
    lower_half = jnp.concatenate([sine_part, cosine], axis=1)
    return jnp.concatenate([upper_half, lower_half], axis=0).astype(jnp.bfloat16)


def quarter_table():
    position = jnp.arange(GX, dtype=jnp.int32)
    phase_step = position[:, None] * position[None, :] % GX
    cosine = jnp.where(phase_step == 0, 1.0, jnp.where(phase_step == 2, -1.0, 0.0)) * 0.5
    sine_part = jnp.where(phase_step == 1, 1.0, jnp.where(phase_step == 3, -1.0, 0.0)) * 0.5
    real_in = jnp.stack([cosine, -sine_part], axis=2)
    imag_in = jnp.stack([sine_part, cosine], axis=2)
    return jnp.stack([real_in, imag_in], axis=1).astype(jnp.float32)


def form_power(voltages, grid_feed):
    row_count = voltages.shape[0] * voltages.shape[1] * voltages.shape[2]
    feed_count = voltages.shape[4]
    gridded = jnp.take(voltages.reshape(row_count, 2, feed_count), grid_feed, axis=2)
    gridded = jnp.transpose(gridded.reshape(row_count, 2, GX, GY), (0, 2, 1, 3)).reshape(
        row_count * GX, 2 * GY
    )
    along_y = jnp.dot(
        gridded, steering_table(GY, 1.0 / math.sqrt(GY)), preferred_element_type=jnp.float32
    ).astype(jnp.bfloat16)
    along_y = along_y.reshape(row_count, GX, 2, GY).astype(jnp.float32)
    formed = jnp.einsum(
        "rgpy,gpbq->rbqy", along_y, quarter_table(), precision=lax.Precision.HIGHEST
    )
    intensity = 0.5 * (formed[:, :, 0, :] ** 2 + formed[:, :, 1, :] ** 2)
    return intensity.astype(jnp.bfloat16).reshape(row_count, feed_count)


def body(voltages, grid_feed, delays):
    band_count, sub_local, time_local = (voltages.shape[0], voltages.shape[1], voltages.shape[2])
    feed_count = voltages.shape[4]
    columns = lax.axis_size("beam")
    col_width = feed_count // columns
    intensity = form_power(voltages, grid_feed).reshape(
        band_count, sub_local, time_local, columns, col_width
    )
    regrouped = jnp.transpose(intensity, (0, 3, 1, 2, 4)).reshape(
        band_count * columns, sub_local, time_local, col_width
    )
    turned = lax.all_to_all(regrouped, ("freq", "beam"), split_axis=0, concat_axis=1, tiled=True)
    turned = turned.reshape(-1, time_local, col_width)
    full_time = lax.all_gather(turned, "dm", axis=1, tiled=True)
    sub_count, total_time = (full_time.shape[0], full_time.shape[1])
    levels = full_time.astype(jnp.float32)
    centered = (levels - jnp.mean(levels, axis=1, keepdims=True)).astype(jnp.bfloat16)
    flattened = centered.reshape(sub_count * total_time, col_width)
    out_time = total_time // 2
    offsets = jnp.arange(out_time, dtype=jnp.int32)
    sample_ids = jnp.arange(total_time, dtype=jnp.int32)
    dm_local = delays.shape[2]
    dm_block = 32
    lag_blocks = jnp.transpose(delays[0]).reshape(dm_local // dm_block, dm_block, sub_count)

    def dedisperse(lag_rows):
        shifted = offsets[None, :, None] + lag_rows[:, None, :]
        selector = (shifted[:, :, :, None] == sample_ids[None, None, None, :]).astype(jnp.bfloat16)
        summed = jnp.dot(
            selector.reshape(dm_block * out_time, sub_count * total_time),
            flattened,
            preferred_element_type=jnp.float32,
        )
        return summed.reshape(dm_block, out_time, col_width)

    partial_sum = lax.map(dedisperse, lag_blocks).reshape(dm_local, out_time, col_width)
    cumulative = lax.all_to_all(
        jnp.cumsum(
            lax.all_to_all(partial_sum[None], "freq", split_axis=1, concat_axis=0, tiled=True),
            axis=0,
        ),
        "freq",
        split_axis=0,
        concat_axis=1,
        tiled=True,
    )
    return cumulative * (1.0 / math.sqrt(FREQS))


def solution(mesh):
    in_specs = (P(None, ("freq", "beam"), ("grp", "dm"), None, None), P(), P("freq", None, "dm"))
    out_specs = P("freq", "dm", "grp", "beam")
    return jax.shard_map(body, mesh=mesh, in_specs=in_specs, out_specs=out_specs, check_vma=False)
```

profile of v0, /device:TPU:0, one launch (start us, length us, event | category | flops | bytes accessed | tf_op | source)
XLA Modules:
  0.0 787.1 jit_solution(15443421244380062521)
XLA Ops:
  6.6 1.1 negate_convert_fusion
  7.7 0.7 fusion.43
  8.4 0.7 compare_and_fusion
  9.1 1.0 fusion.40
  10.1 0.1 copy.58
  10.2 0.1 copy.59
  10.3 56.0 %copy.60 = bf16[4096,2,1024]{0,1,2:T(2,128)(2,1)} copy(bf16[4096,2,1024]{2,1,0:T(2,128)(2,1)} %bitcast.78) | data formatting | bytes 33554432 | tf_op jit(solution)/shard_map/reshape | solution.py:36
  66.3 66.2 %gather_fusion = bf16[1024,4096,2]{1,2,0:T(2,128)(2,1)} fusion(bf16[4096,2,1024]{0,1,2:T(2,128)(2,1)} %copy.60, s32[1024]{0:T(1024)S(1)} %fusion.43), kind=kCustom, calls=%fused_computation | custom fusion | bytes 33558528 | tf_op jit(solution)/shard_map/jit(_take)/gather | solution.py:36
  132.5 56.3 %copy.61 = bf16[4096,2,4,256]{3,1,2,0:T(2,128)(2,1)} copy(bf16[4096,2,4,256]{0,1,3,2:T(2,128)(2,1)} %bitcast.75) | data formatting | bytes 33554432 | tf_op jit(solution)/shard_map/jit(_take)/gather | solution.py:36
  188.8 16.6 %broadcast_select_fusion = bf16[4096,2,4,256]{3,1,2,0:T(2,128)(2,1)S(1)} fusion(bf16[4096,2,4,256]{3,1,2,0:T(2,128)(2,1)} %copy.61, pred[4,256]{1,0:T(4,128)(4,1)S(1)} %broadcast_in_dim.47), kind=kLoop, calls=%fused_computation.15 | loop fusion | flops 8388608 | bytes 33555456 | tf_op jit(solution)/shard_map/jit(_take)/select_n | solution.py:36
  205.4 10.7 %copy.80 = bf16[2048,8,2,256]{3,1,2,0:T(8,128)(2,1)} copy(bf16[2048,8,2,256]{3,2,1,0:T(2,128)(2,1)S(1)} %bitcast.74) | data formatting | bytes 33554432
  216.0 20.0 %convolution_convert_fusion = bf16[16384,512]{1,0:T(8,128)(2,1)} fusion(bf16[16384,512]{1,0:T(8,128)(2,1)} %bitcast.79, bf16[256,256]{1,0:T(8,128)(2,1)S(1)} %get-tuple-element.76, bf16[256,256]{1,0:T(8,128)(2,1)S(1)} %fusion.40, bf16[256,256]{1,0:T(8,128)(2,1)S(1)} %get-tuple-element.75), kind=kOutput, calls=%fused_computation.16 | convolution fusion | flops 8600420352 | bytes 33947648 | tf_op jit(solution)/shard_map/dot_general | solution.py:40
  236.1 23.9 %reshape.188 = bf16[4096,4,2,256]{3,2,1,0:T(2,128)(2,1)} reshape(bf16[16384,512]{1,0:T(8,128)(2,1)} %convolution_convert_fusion) | data formatting | bytes 33554432 | tf_op jit(solution)/shard_map/reshape | solution.py:43
  259.9 45.2 %fusion.22 = f32[4096,4,2,256]{3,1,0,2:T(4,128)} fusion(bf16[4096,4,2,256]{3,2,1,0:T(2,128)(2,1)} %reshape.188, f32[4,1,4,2]{0,2,1,3:T(4,128)S(1)} %copy.59, f32[4,1,4,2]{0,2,1,3:T(4,128)S(1)} %copy.58), kind=kOutput, calls=%fused_computation.26 | convolution fusion | flops 805306432 | bytes 50331904 | tf_op jit(solution)/shard_map/rgpy,gpbq->rbqy/dot_general | solution.py:44
  305.1 16.6 %fusion.18 = bf16[4096,4,1,256]{3,1,0,2:T(4,128)(2,1)} fusion(f32[4096,4,2,256]{3,1,0,2:T(4,128)} %fusion.22), kind=kLoop, calls=%fused_computation.21 | loop fusion | flops 20971520 | bytes 41943040 | tf_op jit(solution)/shard_map/convert_element_type | solution.py:48
  321.7 18.1 %convert_element_type.31 = bf16[4,256,4,2,512]{4,3,2,1,0:T(2,128)(2,1)} reshape(bf16[4096,4,1,256]{3,1,0,2:T(4,128)(2,1)} %fusion.18) | data formatting | bytes 16777216 | tf_op jit(solution)/shard_map/convert_element_type | solution.py:48
  339.8 9.8 %copy.63 = bf16[4,256,4,2,512]{4,1,2,3,0:T(8,128)(2,1)} copy(bf16[4,256,4,2,512]{4,3,2,1,0:T(2,128)(2,1)} %convert_element_type.31) | data formatting | bytes 16777216 | tf_op jit(solution)/shard_map/convert_element_type | solution.py:48
  349.6 190.6 %all_to_all.30 = bf16[8,256,4,512]{3,1,2,0:T(8,128)(2,1)} all-to-all(bf16[8,256,4,512]{3,1,2,0:T(8,128)(2,1)} %bitcast.77), channel_id=1, replica_groups=mesh['grp'=2,'freq'=4,'beam'=2,'dm'=2] {'freq','beam'}, dimensions={0} | all-to-all | bytes 16777216 | tf_op jit(solution)/shard_map/all_to_all | solution.py:62
  540.3 7.6 copy.64
  547.9 0.3 copy.57
  548.2 29.0 %all-gather.2.cloned.1.call-done = bf16[2048,8,512]{2,0,1:T(8,128)(2,1)} async-done(((bf16[2048,4,512]{2,0,1:T(8,128)(2,1)}), bf16[2048,8,512]{2,0,1:T(8,128)(2,1)}) %all-gather.2.cloned.1.call-update) | async-done | bytes 16777232 | tf_op jit(solution)/shard_map/all_gather | solution.py:64
  577.2 20.3 %convert_reduce_fusion = f32[2048,512]{1,0:T(8,128)S(1)} fusion(bf16[2048,8,512]{2,0,1:T(8,128)(2,1)} %all-gather.2.cloned.1.call-done), kind=kLoop, calls=%fused_computation.13 | loop fusion | flops 15728640 | bytes 20971520 | tf_op jit(solution)/shard_map/reduce_sum | solution.py:67
  597.6 0.5 broadcast_multiply_fusion
  598.1 43.1 %fusion.15 = bf16[16384,512]{1,0:T(8,128)(2,1)} fusion(f32[2048,512]{1,0:T(8,128)S(1)} %broadcast_multiply_fusion, bf16[2048,8,512]{2,0,1:T(8,128)(2,1)S(1)} %copy-done), kind=kLoop, calls=%fused_computation.17 | loop fusion | flops 25165824 | bytes 37748736 | tf_op jit(solution)/shard_map/reshape | solution.py:68
  641.2 76.5 %while.11 = (s32[]{:T(128)}, f32[4,32,4,512]{3,1,0,2:T(8,128)S(1)}, s32[4,32,2048]{2,1,0:T(8,128)S(1)}, bf16[16384,512]{1,0:T(8,128)(2,1)}, s32[]{:T(128)}) while((s32[]{:T(128)}, f32[4,32,4,512]{3,1,0,2:T(8,128)S(1)}, s32[4,32,2048]{2,1,0:T(8,128)S(1)}, bf16[16384,512]{1,0:T(8,128)(2,1)}, s32[]{:T(128)}) %tuple.33), condition=%wide.region_2.3_spmd.clone, body=%wide.region_1.2_spmd.clone.sunk | while | flops 2149842944 | bytes 20709444 | solution.py:86
  641.2 0.3 copy.93
  641.5 2.2 iota_add_fusion.2
  643.8 0.1 iota.55
  643.8 0.5 eq.131
  644.3 15.9 %fusion.52 = f32[4,32,4,512]{3,1,0,2:T(8,128)S(1)} fusion(f32[4,32,4,512]{3,1,0,2:T(8,128)S(1)} %get-tuple-element.110, s32[]{:T(128)} %get-tuple-element.109, bf16[16384,512]{1,0:T(8,128)(2,1)} %get-tuple-element.117, s32[16384]{0:T(1024)S(1)} %eq.131, s32[32,4,2048]{0,2,1:T(8,128)} %iota_add_fusion.2), kind=kOutput, calls=%fused_computation.10.clone.1 | convolution fusion | flops 2149580800 | bytes 18153476 | tf_op jit(solution)/shard_map/while/body/eval_jaxpr/dot_general | solution.py:79
  660.3 0.3 copy.93
  660.7 2.2 iota_add_fusion.2
  663.0 0.5 eq.131
  663.5 16.0 %fusion.52 = f32[4,32,4,512]{3,1,0,2:T(8,128)S(1)} fusion(f32[4,32,4,512]{3,1,0,2:T(8,128)S(1)} %get-tuple-element.110, s32[]{:T(128)} %get-tuple-element.109, bf16[16384,512]{1,0:T(8,128)(2,1)} %get-tuple-element.117, s32[16384]{0:T(1024)S(1)} %eq.131, s32[32,4,2048]{0,2,1:T(8,128)} %iota_add_fusion.2), kind=kOutput, calls=%fused_computation.10.clone.1 | convolution fusion | flops 2149580800 | bytes 18153476 | tf_op jit(solution)/shard_map/while/body/eval_jaxpr/dot_general | solution.py:79
  679.5 0.3 copy.93
  679.8 2.2 iota_add_fusion.2
  682.1 0.5 eq.131
  682.6 16.0 %fusion.52 = f32[4,32,4,512]{3,1,0,2:T(8,128)S(1)} fusion(f32[4,32,4,512]{3,1,0,2:T(8,128)S(1)} %get-tuple-element.110, s32[]{:T(128)} %get-tuple-element.109, bf16[16384,512]{1,0:T(8,128)(2,1)} %get-tuple-element.117, s32[16384]{0:T(1024)S(1)} %eq.131, s32[32,4,2048]{0,2,1:T(8,128)} %iota_add_fusion.2), kind=kOutput, calls=%fused_computation.10.clone.1 | convolution fusion | flops 2149580800 | bytes 18153476 | tf_op jit(solution)/shard_map/while/body/eval_jaxpr/dot_general | solution.py:79
  698.6 0.3 copy.93
  699.0 2.2 iota_add_fusion.2
  701.3 0.5 eq.131
  701.8 16.0 %fusion.52 = f32[4,32,4,512]{3,1,0,2:T(8,128)S(1)} fusion(f32[4,32,4,512]{3,1,0,2:T(8,128)S(1)} %get-tuple-element.110, s32[]{:T(128)} %get-tuple-element.109, bf16[16384,512]{1,0:T(8,128)(2,1)} %get-tuple-element.117, s32[16384]{0:T(1024)S(1)} %eq.131, s32[32,4,2048]{0,2,1:T(8,128)} %iota_add_fusion.2), kind=kOutput, calls=%fused_computation.10.clone.1 | convolution fusion | flops 2149580800 | bytes 18153476 | tf_op jit(solution)/shard_map/while/body/eval_jaxpr/dot_general | solution.py:79
  717.7 0.7 copy.68
  718.4 30.8 %all_to_all.31 = f32[1,128,4,512]{3,2,0,1:T(4,128)S(1)} all-to-all(f32[1,128,4,512]{3,2,0,1:T(4,128)S(1)} %copy.68), channel_id=1, replica_groups=mesh['grp'=2,'freq'=4,'beam'=2,'dm'=2] {'freq'}, dimensions={1} | all-to-all | bytes 2097152 | tf_op jit(solution)/shard_map/all_to_all | solution.py:89
  749.3 0.9 fusion.25
  750.2 27.9 %all_to_all.32 = f32[4,32,4,512]{3,1,2,0:T(8,128)S(1)} all-to-all(f32[4,32,4,512]{3,1,2,0:T(8,128)S(1)} %fusion.25), channel_id=1, replica_groups=mesh['grp'=2,'freq'=4,'beam'=2,'dm'=2] {'freq'}, dimensions={0} | all-to-all | bytes 2097152 | tf_op jit(solution)/shard_map/all_to_all | solution.py:87
  778.1 0.2 copy_multiply_fusion
  778.2 1.6 copy.71
  (18 shorter events, 0.4 us)
Async XLA Ops:
  6.5 570.7 %all-gather.2.cloned.1.call-start = ((), (), s32[]{:S(2)}) async-start(), calls=%async_computation.3 | async-start | bytes 25165824 | tf_op jit(solution)/shard_map/all_gather | solution.py:64
  540.3 7.6 copy-start.1
  577.2 20.8 %copy-start = (bf16[2048,8,512]{2,0,1:T(8,128)(2,1)S(1)}, bf16[2048,8,512]{2,0,1:T(8,128)(2,1)}, u32[]{:S(2)}) copy-start(bf16[2048,8,512]{2,0,1:T(8,128)(2,1)} %all-gather.2.cloned.1.call-done) | copy-start | bytes 50331652
Sparse Core Ops, SparseCore 0:
  548.0 29.1 all-gather.1
where the time goes:
time: 800 us; the launch traced here: 787 us
  local copies, waits for them, and re-layouts  255 us (32%)
  blocking collectives  249 us (31%)
  matrix products  129 us (16%)
  other arithmetic  111 us (14%)
  waiting for transfers between devices  29 us (4%)
  between operations  13.9 us (2%)
    all_to_all x1, blocking collectives, body(): lax.all_to_all(regrouped, ('freq', 'beam'), split_axis=0, concat_axis=1,...  191 us
    gather x2, local copies, waits for them, and re-layouts, form_power(): jnp.take(voltages.reshape(row_count, 2, feed_count), grid_feed, axis=2)  122 us
    dot_general x4, matrix products, dedisperse(): jnp.dot(selector.reshape(dm_block * out_time, sub_count * total_time), fl...  63.8 us
    reshape x1, local copies, waits for them, and re-layouts, form_power(): voltages.reshape(row_count, 2, feed_count)  56 us
    dot_general x1, matrix products, form_power(): jnp.einsum('rgpy,gpbq->rbqy', along_y, quarter_table(), precision=lax.Pre...  45.2 us
    reshape x1, other arithmetic, body(): flattened = centered.reshape(sub_count * total_time, col_width)  43.1 us
    all_to_all x1, blocking collectives, body(): lax.all_to_all(partial_sum[None], 'freq', split_axis=1, concat_axis=0, ti...  30.8 us
    all_gather x1, waiting for transfers between devices, body(): full_time = lax.all_gather(turned, 'dm', axis=1, tiled=True)  29 us
  transfers between devices with their start and end apart: 1, of which 1 were waited for; matrix products, arithmetic and copies ran while one was open for 0% of the time, Pallas kernels for 0%

commit v1 on v0

--- a/solution.py
+++ b/solution.py
@@ -7,6 +7,17 @@
 GX = 4
 GY = 256
 FREQS = 8192
+
+
+def in_blocks(array, dim, size):
+    before, after = (array.shape[:dim], array.shape[dim + 1 :])
+    return jnp.moveaxis(array.reshape(*before, size, -1, *after), dim, 0)
+
+
+def laid_out(blocks, dim):
+    blocks = jnp.moveaxis(blocks, 0, dim)
+    dims = blocks.shape
+    return blocks.reshape(*dims[:dim], dims[dim] * dims[dim + 1], *dims[dim + 2 :])
 
 
 def steering_table(length, factor):
@@ -84,16 +95,18 @@
         return summed.reshape(dm_block, out_time, col_width)
 
     partial_sum = lax.map(dedisperse, lag_blocks).reshape(dm_local, out_time, col_width)
-    cumulative = lax.all_to_all(
-        jnp.cumsum(
-            lax.all_to_all(partial_sum[None], "freq", split_axis=1, concat_axis=0, tiled=True),
-            axis=0,
-        ),
-        "freq",
-        split_axis=0,
-        concat_axis=1,
-        tiled=True,
+    array = jnp.cumsum(
+        lax.all_to_all(partial_sum[None], "freq", split_axis=1, concat_axis=0, tiled=True), axis=0
     )
+    size, position_2 = (lax.axis_size("freq"), lax.axis_index("freq"))
+    blocks = in_blocks(array, 0, size)
+    out = blocks
+    for step in range(1, size):
+        target, source = ((position_2 + step) % size, (position_2 - step) % size)
+        sent = lax.dynamic_index_in_dim(blocks, target, 0)
+        received = lax.ppermute(sent, "freq", [(i, (i + step) % size) for i in range(size)])
+        out = lax.dynamic_update_slice_in_dim(out, received, source, axis=0)
+    cumulative = laid_out(out, 1)
     return cumulative * (1.0 / math.sqrt(FREQS))
 
 

time: 800 us -> 795 us (level)
  blocking collectives: 249 us -> 191 us
  waiting for transfers between devices: 29 us -> 71.9 us
  starting transfers between devices: 0.01 us -> 8.74 us
    all_to_all x2 -> x0, blocking collectives: 58.7 us -> none  [the longest x1 30.8 us: body(): lax.all_to_all(partial_sum[None], 'freq', split_axis=1, concat_axis=0, ti...]
    all_to_all x0 -> x1, waiting for transfers between devices: none -> 26.2 us  [body(): lax.all_to_all(partial_sum[None], 'freq', split_axis=1, concat_axis=0, ti...]
    ppermute x0 -> x3, waiting for transfers between devices: none -> 16.7 us  [body(): lax.ppermute(sent, 'freq', [(i, (i + step) % size) for i in range(size)])]
  transfers between devices with their start and end apart: 1 -> 5, of which waited for: 1 -> 4; matrix products, arithmetic and copies ran while one was open for 0% -> 0% of each run, Pallas kernels for 0% -> 0%
where the time goes in v1:
time: 795 us; the launch traced here: 780 us
  local copies, waits for them, and re-layouts  255 us (32%)
  blocking collectives  191 us (24%)
  matrix products  129 us (16%)
  other arithmetic  111 us (14%)
  waiting for transfers between devices  71.9 us (9%)
  between operations  13.9 us (2%)
  starting transfers between devices  8.74 us (1%)
    all_to_all x1, blocking collectives, body(): lax.all_to_all(regrouped, ('freq', 'beam'), split_axis=0, concat_axis=1,...  191 us
    gather x2, local copies, waits for them, and re-layouts, form_power(): jnp.take(voltages.reshape(row_count, 2, feed_count), grid_feed, axis=2)  123 us
    dot_general x4, matrix products, dedisperse(): jnp.dot(selector.reshape(dm_block * out_time, sub_count * total_time), fl...  63.8 us
    reshape x1, local copies, waits for them, and re-layouts, form_power(): voltages.reshape(row_count, 2, feed_count)  56 us
    dot_general x1, matrix products, form_power(): jnp.einsum('rgpy,gpbq->rbqy', along_y, quarter_table(), precision=lax.Pre...  45.2 us
    reshape x1, other arithmetic, body(): flattened = centered.reshape(sub_count * total_time, col_width)  43.1 us
    all_gather x1, waiting for transfers between devices, body(): full_time = lax.all_gather(turned, 'dm', axis=1, tiled=True)  29 us
    convert_element_type x2, local copies, waits for them, and re-layouts, form_power(): return intensity.astype(jnp.bfloat16).reshape(row_count, feed_count)  28 us
  transfers between devices with their start and end apart: 5, of which 4 were waited for; matrix products, arithmetic and copies ran while one was open for 0% of the time, Pallas kernels for 0%

profile of v1, /device:TPU:0, one launch (start us, length us, event | category | flops | bytes accessed | tf_op | source)
XLA Modules:
  0.0 780.0 jit_solution(11331995818257744149)
XLA Ops:
  6.6 1.1 negate_convert_fusion
  7.7 0.7 fusion.41
  8.4 0.7 compare_and_fusion
  9.1 1.0 fusion.38
  10.3 56.0 %copy.46 = bf16[4096,2,1024]{0,1,2:T(2,128)(2,1)} copy(bf16[4096,2,1024]{2,1,0:T(2,128)(2,1)} %bitcast.86) | data formatting | bytes 33554432 | tf_op jit(solution)/shard_map/reshape | solution.py:47
  66.3 66.3 %gather_fusion = bf16[1024,4096,2]{1,2,0:T(2,128)(2,1)} fusion(bf16[4096,2,1024]{0,1,2:T(2,128)(2,1)} %copy.46, s32[1024]{0:T(1024)S(1)} %fusion.41), kind=kCustom, calls=%fused_computation | custom fusion | bytes 33558528 | tf_op jit(solution)/shard_map/jit(_take)/gather | solution.py:47
  132.5 56.3 %copy.47 = bf16[4096,2,4,256]{3,1,2,0:T(2,128)(2,1)} copy(bf16[4096,2,4,256]{0,1,3,2:T(2,128)(2,1)} %bitcast.83) | data formatting | bytes 33554432 | tf_op jit(solution)/shard_map/jit(_take)/gather | solution.py:47
  188.9 16.6 %broadcast_select_fusion = bf16[4096,2,4,256]{3,1,2,0:T(2,128)(2,1)S(1)} fusion(bf16[4096,2,4,256]{3,1,2,0:T(2,128)(2,1)} %copy.47, pred[4,256]{1,0:T(4,128)(4,1)S(1)} %broadcast_in_dim.47), kind=kLoop, calls=%fused_computation.15 | loop fusion | flops 8388608 | bytes 33555456 | tf_op jit(solution)/shard_map/jit(_take)/select_n | solution.py:47
  205.4 10.7 %copy.63 = bf16[2048,8,2,256]{3,1,2,0:T(8,128)(2,1)} copy(bf16[2048,8,2,256]{3,2,1,0:T(2,128)(2,1)S(1)} %bitcast.82) | data formatting | bytes 33554432
  216.1 20.0 %convolution_convert_fusion = bf16[16384,512]{1,0:T(8,128)(2,1)} fusion(bf16[16384,512]{1,0:T(8,128)(2,1)} %bitcast.87, bf16[256,256]{1,0:T(8,128)(2,1)S(1)} %get-tuple-element.77, bf16[256,256]{1,0:T(8,128)(2,1)S(1)} %fusion.38, bf16[256,256]{1,0:T(8,128)(2,1)S(1)} %get-tuple-element.76), kind=kOutput, calls=%fused_computation.16 | convolution fusion | flops 8600420352 | bytes 33947648 | tf_op jit(solution)/shard_map/dot_general | solution.py:51
  236.2 23.9 %reshape.191 = bf16[4096,4,2,256]{3,2,1,0:T(2,128)(2,1)} reshape(bf16[16384,512]{1,0:T(8,128)(2,1)} %convolution_convert_fusion) | data formatting | bytes 33554432 | tf_op jit(solution)/shard_map/reshape | solution.py:54
  260.1 45.2 %fusion.22 = f32[4096,4,2,256]{3,1,0,2:T(4,128)} fusion(bf16[4096,4,2,256]{3,2,1,0:T(2,128)(2,1)} %reshape.191, f32[4,1,4,2]{0,2,1,3:T(4,128)S(1)} %copy.45, f32[4,1,4,2]{0,2,1,3:T(4,128)S(1)} %copy.44), kind=kOutput, calls=%fused_computation.26 | convolution fusion | flops 805306432 | bytes 50331904 | tf_op jit(solution)/shard_map/rgpy,gpbq->rbqy/dot_general | solution.py:55
  305.2 16.6 %fusion.18 = bf16[4096,4,1,256]{3,1,0,2:T(4,128)(2,1)} fusion(f32[4096,4,2,256]{3,1,0,2:T(4,128)} %fusion.22), kind=kLoop, calls=%fused_computation.21 | loop fusion | flops 20971520 | bytes 41943040 | tf_op jit(solution)/shard_map/convert_element_type | solution.py:59
  321.8 18.1 %convert_element_type.31 = bf16[4,256,4,2,512]{4,3,2,1,0:T(2,128)(2,1)} reshape(bf16[4096,4,1,256]{3,1,0,2:T(4,128)(2,1)} %fusion.18) | data formatting | bytes 16777216 | tf_op jit(solution)/shard_map/convert_element_type | solution.py:59
  340.0 9.8 %copy.49 = bf16[4,256,4,2,512]{4,1,2,3,0:T(8,128)(2,1)} copy(bf16[4,256,4,2,512]{4,3,2,1,0:T(2,128)(2,1)} %convert_element_type.31) | data formatting | bytes 16777216 | tf_op jit(solution)/shard_map/convert_element_type | solution.py:59
  349.8 190.6 %all_to_all.21 = bf16[8,256,4,512]{3,1,2,0:T(8,128)(2,1)} all-to-all(bf16[8,256,4,512]{3,1,2,0:T(8,128)(2,1)} %bitcast.85), channel_id=1, replica_groups=mesh['grp'=2,'freq'=4,'beam'=2,'dm'=2] {'freq','beam'}, dimensions={0} | all-to-all | bytes 16777216 | tf_op jit(solution)/shard_map/all_to_all | solution.py:73
  540.4 7.6 copy.50
  548.0 0.3 copy.43
  548.4 29.0 %all-gather.2.cloned.1.call-done = bf16[2048,8,512]{2,0,1:T(8,128)(2,1)} async-done(((bf16[2048,4,512]{2,0,1:T(8,128)(2,1)}), bf16[2048,8,512]{2,0,1:T(8,128)(2,1)}) %all-gather.2.cloned.1.call-update) | async-done | bytes 16777232 | tf_op jit(solution)/shard_map/all_gather | solution.py:75
  577.4 20.3 %convert_reduce_fusion = f32[2048,512]{1,0:T(8,128)S(1)} fusion(bf16[2048,8,512]{2,0,1:T(8,128)(2,1)} %all-gather.2.cloned.1.call-done), kind=kLoop, calls=%fused_computation.13 | loop fusion | flops 15728640 | bytes 20971520 | tf_op jit(solution)/shard_map/reduce_sum | solution.py:78
  597.7 0.5 broadcast_multiply_fusion
  598.2 43.1 %fusion.15 = bf16[16384,512]{1,0:T(8,128)(2,1)} fusion(f32[2048,512]{1,0:T(8,128)S(1)} %broadcast_multiply_fusion, bf16[2048,8,512]{2,0,1:T(8,128)(2,1)S(1)} %copy-done), kind=kLoop, calls=%fused_computation.17 | loop fusion | flops 25165824 | bytes 37748736 | tf_op jit(solution)/shard_map/reshape | solution.py:79
  641.3 76.5 %while.11 = (s32[]{:T(128)}, f32[4,32,4,512]{3,1,0,2:T(8,128)S(1)}, s32[4,32,2048]{2,1,0:T(8,128)S(1)}, bf16[16384,512]{1,0:T(8,128)(2,1)}, s32[]{:T(128)}) while((s32[]{:T(128)}, f32[4,32,4,512]{3,1,0,2:T(8,128)S(1)}, s32[4,32,2048]{2,1,0:T(8,128)S(1)}, bf16[16384,512]{1,0:T(8,128)(2,1)}, s32[]{:T(128)}) %tuple.34), condition=%wide.region_2.3_spmd.clone, body=%wide.region_1.2_spmd.clone.sunk | while | flops 2149842944 | bytes 20709444 | solution.py:97
  641.4 0.3 copy.73
  641.7 2.2 iota_add_fusion.2
  644.0 0.5 eq.138
  644.5 16.0 %fusion.52 = f32[4,32,4,512]{3,1,0,2:T(8,128)S(1)} fusion(f32[4,32,4,512]{3,1,0,2:T(8,128)S(1)} %get-tuple-element.109, s32[]{:T(128)} %get-tuple-element.108, bf16[16384,512]{1,0:T(8,128)(2,1)} %get-tuple-element.116, s32[16384]{0:T(1024)S(1)} %eq.138, s32[32,4,2048]{0,2,1:T(8,128)} %iota_add_fusion.2), kind=kOutput, calls=%fused_computation.10.clone.1 | convolution fusion | flops 2149580800 | bytes 18153476 | tf_op jit(solution)/shard_map/while/body/eval_jaxpr/dot_general | solution.py:90
  660.5 0.3 copy.73
  660.8 2.2 iota_add_fusion.2
  663.1 0.5 eq.138
  663.6 16.0 %fusion.52 = f32[4,32,4,512]{3,1,0,2:T(8,128)S(1)} fusion(f32[4,32,4,512]{3,1,0,2:T(8,128)S(1)} %get-tuple-element.109, s32[]{:T(128)} %get-tuple-element.108, bf16[16384,512]{1,0:T(8,128)(2,1)} %get-tuple-element.116, s32[16384]{0:T(1024)S(1)} %eq.138, s32[32,4,2048]{0,2,1:T(8,128)} %iota_add_fusion.2), kind=kOutput, calls=%fused_computation.10.clone.1 | convolution fusion | flops 2149580800 | bytes 18153476 | tf_op jit(solution)/shard_map/while/body/eval_jaxpr/dot_general | solution.py:90
  679.6 0.3 copy.73
  680.0 2.2 iota_add_fusion.2
  682.3 0.5 eq.138
  682.8 16.0 %fusion.52 = f32[4,32,4,512]{3,1,0,2:T(8,128)S(1)} fusion(f32[4,32,4,512]{3,1,0,2:T(8,128)S(1)} %get-tuple-element.109, s32[]{:T(128)} %get-tuple-element.108, bf16[16384,512]{1,0:T(8,128)(2,1)} %get-tuple-element.116, s32[16384]{0:T(1024)S(1)} %eq.138, s32[32,4,2048]{0,2,1:T(8,128)} %iota_add_fusion.2), kind=kOutput, calls=%fused_computation.10.clone.1 | convolution fusion | flops 2149580800 | bytes 18153476 | tf_op jit(solution)/shard_map/while/body/eval_jaxpr/dot_general | solution.py:90
  698.8 0.3 copy.73
  699.1 2.2 iota_add_fusion.2
  701.4 0.5 eq.138
  701.9 16.0 %fusion.52 = f32[4,32,4,512]{3,1,0,2:T(8,128)S(1)} fusion(f32[4,32,4,512]{3,1,0,2:T(8,128)S(1)} %get-tuple-element.109, s32[]{:T(128)} %get-tuple-element.108, bf16[16384,512]{1,0:T(8,128)(2,1)} %get-tuple-element.116, s32[16384]{0:T(1024)S(1)} %eq.138, s32[32,4,2048]{0,2,1:T(8,128)} %iota_add_fusion.2), kind=kOutput, calls=%fused_computation.10.clone.1 | convolution fusion | flops 2149580800 | bytes 18153476 | tf_op jit(solution)/shard_map/while/body/eval_jaxpr/dot_general | solution.py:90
  717.9 1.6 copy.54
  719.5 4.9 all-to-all-start.1
  724.4 26.2 %all-to-all-done.1 = f32[1,128,4,512]{3,2,0,1:T(4,128)S(1)} async-done(((f32[1,128,4,512]{3,2,0,1:T(4,128)}), f32[1,128,4,512]{3,2,0,1:T(4,128)S(1)}, u32[]{:S(2)}, u32[]{:S(2)}) %all-to-all-start.1) | async-done | bytes 1048608 | tf_op jit(solution)/shard_map/all_to_all | solution.py:99
  750.6 0.2 fusion.46
  750.9 2.0 collective-permute-start.1
  752.9 1.8 collective-permute-start.2
  754.7 7.2 collective-permute-done
  762.0 9.4 %collective-permute-done.1 = f32[1,1,32,4,512]{4,3,2,0,1:T(4,128)S(1)} collective-permute-done((f32[1,1,32,4,512]{4,3,2,0,1:T(4,128)S(1)}, f32[1,1,32,4,512]{4,3,2,0,1:T(4,128)S(1)}, u32[]{:S(2)}, u32[]{:S(2)}) %collective-permute-start.1) | collective-permute-done | bytes 262176 | tf_op jit(solution)/shard_map/ppermute | solution.py:107
  771.5 1.2 broadcast_multiply_fusion.1
  (27 shorter events, 0.9 us)
Async XLA Ops:
  6.5 570.9 %all-gather.2.cloned.1.call-start = ((), (), s32[]{:S(2)}) async-start(), calls=%async_computation.2 | async-start | bytes 25165824 | tf_op jit(solution)/shard_map/all_gather | solution.py:75
  540.4 7.6 copy-start.1
  577.4 20.8 %copy-start = (bf16[2048,8,512]{2,0,1:T(8,128)(2,1)S(1)}, bf16[2048,8,512]{2,0,1:T(8,128)(2,1)}, u32[]{:S(2)}) copy-start(bf16[2048,8,512]{2,0,1:T(8,128)(2,1)} %all-gather.2.cloned.1.call-done) | copy-start | bytes 50331652
  719.5 31.0 %all-to-all-start.1 = ((f32[1,128,4,512]{3,2,0,1:T(4,128)}), f32[1,128,4,512]{3,2,0,1:T(4,128)S(1)}, u32[]{:S(2)}, u32[]{:S(2)}) async-start(f32[1,128,4,512]{3,2,0,1:T(4,128)} %copy.54), calls=%async_computation.1 | async-start | bytes 2097152 | tf_op jit(solution)/shard_map/all_to_all | solution.py:99
  750.8 11.1 %collective-permute-start = (f32[1,1,32,4,512]{4,3,2,0,1:T(4,128)S(1)}, f32[1,1,32,4,512]{4,3,2,0,1:T(4,128)S(1)}, u32[]{:S(2)}, u32[]{:S(2)}) collective-permute-start(f32[1,1,32,4,512]{4,3,2,0,1:T(4,128)S(1)} %get-tuple-element.71), channel_id=1, source_target_pairs={{0,4},{4,8},{8,12},{12,0},{1,5},{5,9},{9,13},{13,1},{2,6},{6,10},{... | collective-permute-start | bytes 786440 | tf_op jit(solution)/shard_map/ppermute | solution.py:107
  750.9 20.5 %collective-permute-start.1 = (f32[1,1,32,4,512]{4,3,2,0,1:T(4,128)S(1)}, f32[1,1,32,4,512]{4,3,2,0,1:T(4,128)S(1)}, u32[]{:S(2)}, u32[]{:S(2)}) collective-permute-start(f32[1,1,32,4,512]{4,3,2,0,1:T(4,128)S(1)} %get-tuple-element.70), channel_id=1, source_target_pairs={{0,8},{4,12},{8,0},{12,4},{1,9},{5,13},{9,1},{13,5},{2,10},{6,14},... | collective-permute-start | bytes 786440 | tf_op jit(solution)/shard_map/ppermute | solution.py:107
  752.9 18.6 %collective-permute-start.2 = (f32[1,1,32,4,512]{4,3,2,0,1:T(4,128)S(1)}, f32[1,1,32,4,512]{4,3,2,0,1:T(4,128)S(1)}, u32[]{:S(2)}, u32[]{:S(2)}) collective-permute-start(f32[1,1,32,4,512]{4,3,2,0,1:T(4,128)S(1)} %get-tuple-element.69), channel_id=1, source_target_pairs={{0,12},{4,0},{8,4},{12,8},{1,13},{5,1},{9,5},{13,9},{2,14},{6,2},{... | collective-permute-start | bytes 786440 | tf_op jit(solution)/shard_map/ppermute | solution.py:107
Sparse Core Ops, SparseCore 0:
  548.1 29.2 all-gather.1
